TPU v7x, 256 devices: a whole 4x4x8 slice. The times are simulated.
256 devices in a mesh: gx: 8 (over x, core), gy: 4 (over y), gz: 8 (over z).
Axes of the slice: x: 4, y: 4, z: 8, core: 2. Of those that a mesh axis runs over, the one named last changes fastest.
Arguments:
- atom_feat: bfloat16 [262144, 128], P(('gx', 'gy', 'gz')), may hold values from -6 to 6
- atom_env: bfloat16 [262144, 9, 128], P(('gx', 'gy', 'gz')), may hold values from -6 to 6
- export_index: int32 [65536], P(('gx', 'gy', 'gz')), may hold values from 0 to 1023
- pair_vec: float32 [3, 524288], P(None, ('gx', 'gy', 'gz')), may hold values from -8 to 8
- pair_center: int32 [524288], P(('gx', 'gy', 'gz')), may hold values from 0 to 1023
- pair_owner: int32 [524288, 1], P(('gx', 'gy', 'gz')), may hold values from 0 to 31; in each aligned block of 2048 rows (0 to 2047, 2048 to 4095, ...) at most 96 rows name the same one
- pair_neigh: int32 [524288], P(('gx', 'gy', 'gz')), may hold values from 0 to 7935
- pair_count: int32 [256], P(('gx', 'gy', 'gz')), may hold values from 512 to 2048
- center_proj: bfloat16 [128, 512], replicated, may hold values from -0.375 to 0.375
- neighbour_proj: bfloat16 [128, 512], replicated, may hold values from -0.375 to 0.375
- radial_proj: bfloat16 [8, 512], replicated, may hold values from -4 to 4
- hidden_proj: bfloat16 [512, 512], replicated, may hold values from -0.25 to 0.25
- split_proj: bfloat16 [512, 384], replicated, may hold values from -0.5 to 0.5
- scalar_proj: bfloat16 [384, 512], replicated, may hold values from -0.3125 to 0.3125
- path_gain: float32 [3, 128], replicated, may hold values from 0.1 to 1.9
- energy_proj: float32 [512], replicated, may hold values from -0.5 to 0.5
Outputs:
- pair_latent: bfloat16 [524288, 512], P(('gx', 'gy', 'gz'))
- pair_vector: bfloat16 [3, 524288, 128], P(None, ('gx', 'gy', 'gz'))
- atom_energy: float32 [262144], P(('gx', 'gy', 'gz'))
Inputs may be any that keep to these rules, and one draw needn't show every extreme that they name: `pair_owner`: among the pair slots of one device at most 96 name the same owner, a bound that some block reaches of them.
All inputs are finite; a program needn't handle non-finite values.
Results may differ from a plain program's by a relative error of at most 0.0062.
Values may be sent and summed in bfloat16 or wider, within the bound.
A program may use at most 128 MiB of HBM per device.

v0:
```python
import jax
import jax.numpy as jnp
from jax import lax
from jax.sharding import PartitionSpec as P

cutoff = 6.0
root_two = 2.0**0.5
root_three = 3.0**0.5
root_five = 5.0**0.5
root_fifteen = 15.0**0.5


def with_halo(x, sides, width):
    for axis, dim in sides:
        size, length = (lax.axis_size(axis), x.shape[dim])
        up = [(i, (i + 1) % size) for i in range(size)]
        down = [(j, i) for i, j in up]
        last = lax.slice_in_dim(x, length - width, length, axis=dim)
        leading = lax.slice_in_dim(x, 0, width, axis=dim)
        before = lax.ppermute(last, axis, up)
        after = lax.ppermute(leading, axis, down)
        x = jnp.concatenate([before, x, after], axis=dim)
    return x


def side_by_side(arrays, axis, split_dim, concat_dim, along):
    widths = [a.shape[along] for a in arrays]
    both = jnp.concatenate(arrays, axis=along)
    filled = lax.all_to_all(both, axis, split_axis=split_dim, concat_axis=concat_dim, tiled=True)
    return tuple(jnp.split(filled, [sum(widths[:k]) for k in range(1, len(widths))], axis=along))


def pair_block(
    h_center,
    env_center,
    h_neighbour,
    geometry,
    live,
    center_proj,
    neighbour_proj,
    radial_proj,
    hidden_proj,
    split_proj,
    scalar_proj,
    path_gain,
    energy_proj,
):
    channels = h_center.shape[1]
    basis = radial_proj.shape[0]
    length = jnp.sqrt(jnp.sum(geometry * geometry, axis=0))
    unit = geometry / jnp.maximum(length, 1.0)[None, :]
    spacing = cutoff / (basis - 1)
    centres = jnp.arange(basis).astype(geometry.dtype) * spacing
    radial = jnp.exp(-jnp.square((length[:, None] - centres[None, :]) / spacing))
    before = jnp.dot(h_center, center_proj, preferred_element_type=jnp.float32)
    before = before + jnp.dot(h_neighbour, neighbour_proj, preferred_element_type=jnp.float32)
    before = before + jnp.dot(
        radial, radial_proj.astype(jnp.float32), precision=lax.Precision.HIGHEST
    )
    hidden = jax.nn.silu(before).astype(jnp.bfloat16)
    latent = jax.nn.silu(jnp.dot(hidden, hidden_proj, preferred_element_type=jnp.float32)).astype(
        jnp.bfloat16
    )
    mixed = jnp.dot(latent, split_proj, preferred_element_type=jnp.float32)
    scalar_part = mixed[:, :channels]
    vector_part = mixed[:, channels : 2 * channels]
    tensor_part = mixed[:, 2 * channels :]
    ux, uy, uz = (unit[0][:, None], unit[1][:, None], unit[2][:, None])
    first = [root_three * ux, root_three * uy, root_three * uz]
    second = [
        root_fifteen * ux * uy,
        root_fifteen * uy * uz,
        0.5 * root_five * (2.0 * uz * uz - ux * ux - uy * uy),
        root_fifteen * ux * uz,
        0.5 * root_fifteen * (ux * ux - uy * uy),
    ]
    env_scalar = env_center[:, 0, :].astype(jnp.float32)
    env_vector = [env_center[:, 1 + m, :].astype(jnp.float32) for m in range(3)]
    env_tensor = [env_center[:, 4 + m, :].astype(jnp.float32) for m in range(5)]
    edge_vector = [vector_part * first[m] for m in range(3)]
    vector_dot = (
        edge_vector[0] * env_vector[0]
        + edge_vector[1] * env_vector[1]
        + edge_vector[2] * env_vector[2]
    )
    tensor_dot = tensor_part * second[0] * env_tensor[0]
    for m in range(1, 5):
        tensor_dot = tensor_dot + tensor_part * second[m] * env_tensor[m]
    invariants = jnp.concatenate(
        [scalar_part * env_scalar, vector_dot / root_three, tensor_dot / root_five], axis=1
    ).astype(jnp.bfloat16)
    update = jax.nn.silu(jnp.dot(invariants, scalar_proj, preferred_element_type=jnp.float32))
    latent_out = jnp.where(live[:, None], latent.astype(jnp.float32) + update, 0.0).astype(
        jnp.bfloat16
    )
    cross = [
        edge_vector[1] * env_vector[2] - edge_vector[2] * env_vector[1],
        edge_vector[2] * env_vector[0] - edge_vector[0] * env_vector[2],
        edge_vector[0] * env_vector[1] - edge_vector[1] * env_vector[0],
    ]
    outputs = []
    for m in range(3):
        value = (
            path_gain[0][None, :] * scalar_part * env_vector[m]
            + path_gain[1][None, :] * edge_vector[m] * env_scalar
            + path_gain[2][None, :] * cross[m] / root_two
        )
        outputs.append(jnp.where(live[:, None], value, 0.0).astype(jnp.bfloat16))
    vector_out = jnp.stack(outputs)
    energy = jnp.sum(latent_out.astype(jnp.float32) * energy_proj[None, :], axis=1)
    energy = jnp.where(live, energy, 0.0)
    return (latent_out, vector_out, energy)


def local(
    atom_feat,
    atom_env,
    export_index,
    pair_vec,
    pair_center,
    pair_owner,
    pair_neigh,
    pair_count,
    center_proj,
    neighbour_proj,
    radial_proj,
    hidden_proj,
    split_proj,
    scalar_proj,
    path_gain,
    energy_proj,
):
    atoms_here = atom_feat.shape[0]
    pair_slots = pair_center.shape[0]
    channels = atom_feat.shape[1]
    owners = lax.axis_size("gy") * lax.axis_size("gz")
    capacity = 3 * pair_slots // (2 * owners)
    exported = atom_feat[export_index]
    shell = with_halo(exported[None, None, None], (("gx", 0), ("gy", 1), ("gz", 2)), 1)
    table = jnp.concatenate([atom_feat, shell.reshape(-1, channels)], axis=0)
    owner = pair_owner[:, 0]
    positions = jnp.arange(pair_slots, dtype=jnp.int32)
    member_of = jnp.arange(owners, dtype=jnp.int32)[:, None] == owner[None, :]
    strictly_before = (positions[:, None] < positions[None, :]).astype(jnp.bfloat16)
    earlier = jnp.dot(
        member_of.astype(jnp.bfloat16), strictly_before, preferred_element_type=jnp.float32
    )
    rank = jnp.sum(jnp.where(member_of, earlier, 0.0), axis=0).astype(jnp.int32)
    slot = owner * capacity + rank
    live = positions < pair_count[0]
    coded = (
        jnp.full((owners * capacity,), -1, jnp.int32).at[slot].set(jnp.where(live, pair_center, -1))
    )
    neigh_codes = jnp.zeros((owners * capacity,), jnp.int32).at[slot].set(pair_neigh)
    placed = jnp.zeros((3, owners * capacity), jnp.float32).at[:, slot].set(pair_vec)
    coded_in, neigh_in, placed_in = (
        *side_by_side(
            (coded.reshape(1, owners, capacity), neigh_codes.reshape(1, owners, capacity)),
            ("gy", "gz"),
            1,
            1,
            0,
        ),
        lax.all_to_all(
            placed.reshape(3, owners, capacity),
            ("gy", "gz"),
            split_axis=1,
            concat_axis=1,
            tiled=True,
        ),
    )
    codes = coded_in.reshape(-1)
    valid = codes >= 0
    center_rows = jnp.maximum(codes, 0)
    geometry = placed_in.reshape(3, owners * capacity)
    latent_far, vector_far, energy_far = pair_block(
        atom_feat[center_rows],
        atom_env[center_rows],
        table[neigh_in.reshape(-1)],
        geometry,
        valid,
        center_proj,
        neighbour_proj,
        radial_proj,
        hidden_proj,
        split_proj,
        scalar_proj,
        path_gain,
        energy_proj,
    )
    atom_energy = jax.ops.segment_sum(energy_far, center_rows, num_segments=atoms_here)
    back_latent, back_vector = (
        lax.all_to_all(
            latent_far.reshape(1, owners, capacity, -1),
            ("gy", "gz"),
            split_axis=1,
            concat_axis=1,
            tiled=True,
        ),
        lax.all_to_all(
            vector_far.reshape(3, owners, capacity, channels),
            ("gy", "gz"),
            split_axis=1,
            concat_axis=1,
            tiled=True,
        ),
    )
    latent_out = back_latent.reshape(owners * capacity, -1)[slot]
    vector_out = back_vector.reshape(3, owners * capacity, channels)[:, slot]
    return (latent_out, vector_out, atom_energy)


def solution(mesh):
    placed = (
        P(("gx", "gy", "gz"), None),
        P(("gx", "gy", "gz"), None, None),
        P(("gx", "gy", "gz")),
        P(None, ("gx", "gy", "gz")),
        P(("gx", "gy", "gz")),
        P(("gx", "gy", "gz"), None),
        P(("gx", "gy", "gz")),
        P(("gx", "gy", "gz")),
        P(),
        P(),
        P(),
        P(),
        P(),
        P(),
        P(),
        P(),
    )
    return jax.shard_map(
        local,
        mesh=mesh,
        in_specs=placed,
        out_specs=(
            P(("gx", "gy", "gz"), None),
            P(None, ("gx", "gy", "gz"), None),
            P(("gx", "gy", "gz")),
        ),
        check_vma=False,
    )
```

profile of v0, /device:TPU:7, one launch (start us, length us, event | category | flops | bytes accessed | tf_op | source)
XLA Modules:
  0.0 333.8 jit_solution(2690860249928666538)
XLA Ops:
  0.6 0.0 copy-start
  0.6 0.8 compare_select_fusion.2
  1.5 1.7 gather_fusion.1
  3.2 0.7 collective-permute-start.1
  3.9 2.3 collective-permute-start
  6.2 1.8 fusion.42
  8.0 8.2 %scatter_custom_fusion.1 = s32[3072]{0:T(1024)S(1)} fusion(s32[2048]{0:T(1024)S(1)} %bitcast.138, s32[2048]{0:T(1024)} %param.22, s32[]{:T(128)} %constant.21.clone.1), kind=kCustom, calls=%fused_computation.131 | custom fusion | bytes 12800 | tf_op jit(solution)/shard_map/scatter | solution.py:154
  16.2 0.1 reshape.246
  17.0 8.1 %scatter_custom_fusion = s32[3072]{0:T(1024)S(1)} fusion(s32[2048]{0:T(1024)S(1)} %bitcast.139, s32[2048]{0:T(1024)S(1)} %fusion.57, s32[]{:T(128)} %constant.18.clone.1), kind=kCustom, calls=%fused_computation.133 | custom fusion | bytes 12292 | tf_op jit(solution)/shard_map/scatter | solution.py:152
  25.1 0.1 reshape.245
  25.2 0.7 pad_add_fusion
  25.8 11.2 %all-to-all-start = ((s32[2,32,96]{2,0,1:T(2,128)}), s32[2,32,96]{2,0,1:T(2,128)S(1)}, u32[]{:S(2)}, u32[]{:S(2)}) async-start(s32[2,32,96]{2,0,1:T(2,128)} %pad_add_fusion), calls=%async_computation | async-start | bytes 65536 | tf_op jit(solution)/shard_map/all_to_all | solution.py:29
  37.0 0.6 slice_bitcast_fusion.11
  37.6 0.5 convert_multiply_fusion.21
  38.1 1.3 copy.41
  39.5 7.2 %scatter_custom_fusion.2 = f32[3,3072]{0,1:T(8,128)} fusion(s32[2048]{0:T(1024)S(1)} %bitcast.140, f32[2048,3]{1,0:T(8,128)} %copy.41, f32[]{:T(128)} %constant.20.clone.1), kind=kCustom, calls=%fused_computation.93 | custom fusion | bytes 37376 | tf_op jit(solution)/shard_map/scatter | solution.py:155
  46.6 2.5 copy.42
  49.2 9.4 %all-to-all-start.1 = ((f32[3,32,96]{2,0,1:T(4,128)}), f32[3,32,96]{2,0,1:T(4,128)}, u32[]{:S(2)}, u32[]{:S(2)}) async-start(f32[3,32,96]{2,0,1:T(4,128)} %copy.42), calls=%async_computation.1 | async-start | bytes 131072 | tf_op jit(solution)/shard_map/all_to_all | solution.py:164
  58.5 0.7 slice_reduce_fusion
  59.2 0.1 reshape.265
  59.3 0.6 copy-done.11
  59.9 9.1 %gather_fusion = bf16[3072,128]{1,0:T(8,128)(2,1)S(1)} fusion(bf16[1024,128]{1,0:T(8,128)(2,1)S(1)} %copy-done.2, s32[3072]{0:T(1024)S(1)} %broadcast_clamp_fusion.1), kind=kCustom, calls=%fused_computation | custom fusion | bytes 1585152 | tf_op jit(solution)/shard_map/gather | solution.py:177
  69.0 1.4 reshape.248
  70.5 0.7 compare_select_fusion
  71.2 0.6 broadcast_clamp_fusion
  71.8 45.1 %gather_fusion.3 = bf16[3072,9,128]{2,0,1:T(8,128)(2,1)} fusion(bf16[1024,9,128]{2,0,1:T(8,128)(2,1)S(1)} %copy-done, s32[3072]{0:T(1024)S(1)} %broadcast_clamp_fusion.1), kind=kCustom, calls=%fused_computation.3 | custom fusion | bytes 14168064 | tf_op jit(solution)/shard_map/gather | solution.py:178
  116.9 4.6 %fusion.66 = f32[3072,512]{1,0:T(8,128)} fusion(bf16[3072,128]{1,0:T(8,128)(2,1)S(1)} %gather_fusion, bf16[128,512]{1,0:T(8,128)(2,1)} %param.24), kind=kOutput, calls=%fused_computation.147 | convolution fusion | flops 402653184 | bytes 7208960 | tf_op jit(solution)/shard_map/dot_general | solution.py:55
  121.5 0.1 compare_reduce_fusion
  121.5 0.1 ge.11
  121.6 0.9 pad_maximum_fusion.4
  122.5 2.5 collective-permute-start.3
  125.0 0.9 multiply_reduce_fusion.1
  125.9 0.1 sqrt.15
  126.0 0.8 copy.43
  126.8 0.1 reshape.250
  127.0 2.6 collective-permute-done.3
  129.5 3.5 %collective-permute-done.2 = bf16[3,1,1,256,128]{4,3,2,1,0:T(8,128)(2,1)S(1)} collective-permute-done((bf16[3,1,1,256,128]{4,3,2,1,0:T(8,128)(2,1)S(1)}, bf16[3,1,1,256,128]{4,3,2,1,0:T(8,128)(2,1)S(1)}, u32[]{:S(2)}, u32[]{:S(2)}) %collective-permute-start.2) | collective-permute-done | bytes 196640 | tf_op jit(solution)/shard_map/ppermute | solution.py:20
  133.0 0.9 pad_maximum_fusion.3
  133.9 2.5 collective-permute-start.5
  136.5 12.1 %collective-permute-done.5 = bf16[3,3,1,256,128]{4,3,2,1,0:T(8,128)(2,1)S(1)} collective-permute-done((bf16[3,3,1,256,128]{4,3,2,1,0:T(8,128)(2,1)S(1)}, bf16[3,3,1,256,128]{4,3,2,1,0:T(8,128)(2,1)S(1)}, u32[]{:S(2)}, u32[]{:S(2)}) %collective-permute-start.5) | collective-permute-done | bytes 589856 | tf_op jit(solution)/shard_map/ppermute | solution.py:21
  148.6 3.1 collective-permute-done.4
  151.8 1.0 pad_maximum_fusion.2
  152.8 0.1 pad_maximum_fusion.1
  152.9 0.6 copy-done.12
  153.5 9.1 %gather_fusion.2 = bf16[3072,128]{1,0:T(8,128)(2,1)S(1)} fusion(bf16[7936,128]{1,0:T(8,128)(2,1)S(1)} %pad_maximum_fusion.1, s32[3072]{0:T(1024)S(1)} %copy-done.12), kind=kCustom, calls=%fused_computation.2 | custom fusion | bytes 1585152 | tf_op jit(solution)/shard_map/gather | solution.py:179
  162.7 1.0 fusion.67
  163.7 6.5 %multiply_convert_fusion.1 = bf16[3072,512]{1,0:T(8,128)(2,1)S(1)} fusion(f32[3072,512]{1,0:T(8,128)} %fusion.66, f32[3072,512]{1,0:T(8,128)S(1)} %fusion.67, bf16[8,512]{1,0:T(8,128)(2,1)S(1)} %copy-done.23, f32[8]{0:T(128)S(1)} %copy-done.25, f32[3072]{0:T(1024)S(1)} %sqrt.15), kind=kOutput, calls=%fused_computation.15 | convolution fusion | flops 162103296 | bytes 15749152 | tf_op jit(solution)/shard_map/dot_general | solution.py:57
  170.2 0.0 copy-start.7
  170.2 2.7 multiply_convert_fusion
  172.9 1.8 fusion.68
  174.8 4.8 %fusion.27 = (bf16[3072,128]{1,0:T(8,128)(2,1)S(1)}, bf16[3072,128]{1,0:T(8,128)(2,1)S(1)}, bf16[3072,128]{1,0:T(8,128)(2,1)}) fusion(f32[3072,384]{1,0:T(8,128)S(1)} %fusion.68, f32[128]{0:T(128)S(1)} %copy-done.18, f32[128]{0:T(128)S(1)} %copy-done.19, f32[128]{0:T(128)S(1)} %get-tuple-element.34, f32[3072]{0:T(1024)S(1)} %get-tuple-element.31, ...), kind=kLoop, calls=%fused_computation.61 | loop fusion | flops 11403264 | bytes 8692224 | tf_op jit(solution)/shard_map/convert_element_type | solution.py:108
  179.6 3.0 fusion.15
  182.6 1.6 pad_maximum_fusion
  184.2 4.7 %all-to-all-start.3 = ((bf16[3,32,96,128]{3,2,0,1:T(8,128)(2,1)}), bf16[3,32,96,128]{3,2,0,1:T(8,128)(2,1)S(1)}, u32[]{:S(2)}, u32[]{:S(2)}) async-start(bf16[3,32,96,128]{3,2,0,1:T(8,128)(2,1)} %pad_maximum_fusion), calls=%async_computation.3 | async-start | bytes 4718592 | tf_op jit(solution)/shard_map/all_to_all | solution.py:200
  189.0 5.7 %fusion.36 = bf16[3072,128]{1,0:T(8,128)(2,1)S(1)} fusion(f32[3072,384]{1,0:T(8,128)} %copy-done.3, bf16[3072,9,128]{2,0,1:T(8,128)(2,1)} %gather_fusion.3, f32[3072]{0:T(1024)S(1)} %get-tuple-element.29, f32[3072]{0:T(1024)S(1)} %get-tuple-element.32, f32[3072]{0:T(1024)S(1)} %get-tuple-element.28, f32[3072]{0:T(1024)S(1)} %get-tuple-element.27, ...), kind=kLoop, calls=%fused_computation.71 | loop fusion | flops 8257536 | bytes 6352896 | tf_op jit(solution)/shard_map/convert.11
  194.7 5.3 %multiply_reduce_fusion = (f32[3072]{0:T(1024)S(1)}, bf16[3072,512]{1,0:T(8,128)(2,1)}) fusion(f32[512]{0:T(512)S(1)} %copy-done.24, bf16[384,512]{1,0:T(8,128)(2,1)S(1)} %copy-done.22, bf16[3072,128]{1,0:T(8,128)(2,1)S(1)} %fusion.36, bf16[3072,128]{1,0:T(8,128)(2,1)S(1)} %get-tuple-element.20, bf16[3072,128]{1,0:T(8,128)(2,1)S(1)} %copy-done.6, ...), kind=kOutput, calls=%fused_computation.12 | convolution fusion | flops 1232335872 | bytes 9061376 | tf_op jit(solution)/shard_map/dot_general | solution.py:92
  200.0 43.7 %all-to-all-done.3 = bf16[3,32,96,128]{3,2,0,1:T(8,128)(2,1)S(1)} async-done(((bf16[3,32,96,128]{3,2,0,1:T(8,128)(2,1)}), bf16[3,32,96,128]{3,2,0,1:T(8,128)(2,1)S(1)}, u32[]{:S(2)}, u32[]{:S(2)}) %all-to-all-start.3) | async-done | bytes 2359328 | tf_op jit(solution)/shard_map/all_to_all | solution.py:200
  243.8 6.9 %all-to-all-start.2 = ((bf16[1,32,96,512]{3,2,0,1:T(8,128)(2,1)}), bf16[1,32,96,512]{3,2,0,1:T(8,128)(2,1)}, u32[]{:S(2)}, u32[]{:S(2)}) async-start(bf16[1,32,96,512]{3,2,0,1:T(8,128)(2,1)} %bitcast.124), calls=%async_computation.2 | async-start | bytes 6291456 | tf_op jit(solution)/shard_map/all_to_all | solution.py:193
  250.7 22.5 %scatter_custom_fusion.3 = f32[1024]{0:T(1024)} fusion(s32[3072]{0:T(1024)} %copy-done.11, f32[3072]{0:T(1024)S(1)} %broadcast_select_fusion, f32[]{:T(128)} %constant.20.clone.1), kind=kCustom, calls=%fused_computation.138 | custom fusion | flops 3072 | bytes 4608 | tf_op jit(solution)/shard_map/scatter-add | solution.py:191
  273.2 3.3 copy.48
  276.5 8.7 %gather_fusion.5 = bf16[2048,3,128]{2,1,0:T(4,128)(2,1)S(1)} fusion(bf16[3,3072,128]{2,0,1:T(4,128)(2,1)} %bitcast.118, s32[2048]{0:T(1024)S(1)} %broadcast_clamp_fusion.2), kind=kCustom, calls=%fused_computation.5 | custom fusion | bytes 3153920 | tf_op jit(solution)/shard_map/gather | solution.py:209
  285.2 1.4 copy.49
  286.6 35.5 %all-to-all-done.2 = bf16[1,32,96,512]{3,2,0,1:T(8,128)(2,1)} async-done(((bf16[1,32,96,512]{3,2,0,1:T(8,128)(2,1)}), bf16[1,32,96,512]{3,2,0,1:T(8,128)(2,1)}, u32[]{:S(2)}, u32[]{:S(2)}) %all-to-all-start.2) | async-done | bytes 3145760 | tf_op jit(solution)/shard_map/all_to_all | solution.py:193
  322.1 11.7 %gather_fusion.4 = bf16[2048,512]{1,0:T(8,128)(2,1)} fusion(bf16[3072,512]{1,0:T(8,128)(2,1)} %bitcast.25, s32[2048]{0:T(1024)S(1)} %broadcast_clamp_fusion.2), kind=kCustom, calls=%fused_computation.4 | custom fusion | bytes 4202496 | tf_op jit(solution)/shard_map/gather | solution.py:208
  (71 shorter events, 0.3 us)
Async XLA Ops:
  0.6 71.1 %copy-start = (bf16[1024,9,128]{2,0,1:T(8,128)(2,1)S(1)}, bf16[1024,9,128]{2,0,1:T(8,128)(2,1)}, u32[]{:S(2)}) copy-start(bf16[1024,9,128]{2,0,1:T(8,128)(2,1)} %param.17) | copy-start | bytes 7077892
  3.2 118.4 %collective-permute-start.1 = (bf16[1,1,1,256,128]{4,3,2,1,0:T(8,128)(2,1)S(1)}, bf16[1,1,1,256,128]{4,3,2,1,0:T(8,128)(2,1)S(1)}, u32[]{:S(2)}, u32[]{:S(2)}) collective-permute-start(bf16[1,1,1,256,128]{4,3,2,1,0:T(8,128)(2,1)S(1)} %bitcast.125), channel_id=1, source_target_pairs={{32,0},{64,32},{96,64},{128,96},{160,128},{192,160},{224,192},{0,2... | collective-permute-start | bytes 196616 | tf_op jit(solution)/shard_map/ppermute | solution.py:21
  3.9 117.8 %collective-permute-start = (bf16[1,1,1,256,128]{4,3,2,1,0:T(8,128)(2,1)S(1)}, bf16[1,1,1,256,128]{4,3,2,1,0:T(8,128)(2,1)}, u32[]{:S(2)}, u32[]{:S(2)}) collective-permute-start(bf16[1,1,1,256,128]{4,3,2,1,0:T(8,128)(2,1)S(1)} %bitcast.126), channel_id=1, source_target_pairs={{0,32},{32,64},{64,96},{96,128},{128,160},{160,192},{192,224},{224... | collective-permute-start | bytes 196616 | tf_op jit(solution)/shard_map/ppermute | solution.py:20
  6.2 1.8 copy-start.16
  6.2 10.8 %copy-start.17 = (s32[2048]{0:T(1024)S(1)}, s32[2048]{0:T(1024)}, u32[]{:S(2)}) copy-start(s32[2048]{0:T(1024)} %param.20) | copy-start | bytes 24580
  6.2 30.9 %copy-start.20 = (f32[3,128]{1,0:T(4,128)S(1)}, f32[3,128]{1,0:T(4,128)}, u32[]{:S(2)}) copy-start(f32[3,128]{1,0:T(4,128)} %param.30) | copy-start | bytes 4612
  6.2 32.0 %copy-start.13 = (f32[3,2048]{1,0:T(4,128)S(1)}, f32[3,2048]{1,0:T(4,128)}, u32[]{:S(2)}) copy-start(f32[3,2048]{1,0:T(4,128)} %param.19) | copy-start | bytes 73732
  8.0 41.2 %copy-start.14 = (s32[2048,1]{0,1:T(1,128)}, s32[2048,1]{0,1:T(1,128)S(1)}, u32[]{:S(2)}) copy-start(s32[2048,1]{0,1:T(1,128)S(1)} %compare_select_fusion.1) | copy-start | bytes 24580
  25.8 23.3 %all-to-all-start = ((s32[2,32,96]{2,0,1:T(2,128)}), s32[2,32,96]{2,0,1:T(2,128)S(1)}, u32[]{:S(2)}, u32[]{:S(2)}) async-start(s32[2,32,96]{2,0,1:T(2,128)} %pad_add_fusion), calls=%async_computation | async-start | bytes 65536 | tf_op jit(solution)/shard_map/all_to_all | solution.py:29
  39.5 20.4 %copy-start.2 = (bf16[1024,128]{1,0:T(8,128)(2,1)S(1)}, bf16[1024,128]{1,0:T(8,128)(2,1)}, u32[]{:S(2)}) copy-start(bf16[1024,128]{1,0:T(8,128)(2,1)} %param.16) | copy-start | bytes 786436
  49.2 10.1 %copy-start.8 = (s32[2,32,96]{2,0,1:T(2,128)}, s32[2,32,96]{2,0,1:T(2,128)S(1)}, u32[]{:S(2)}) copy-start(s32[2,32,96]{2,0,1:T(2,128)S(1)} %all-to-all-done) | copy-start | bytes 73732
  49.2 75.8 %all-to-all-start.1 = ((f32[3,32,96]{2,0,1:T(4,128)}), f32[3,32,96]{2,0,1:T(4,128)}, u32[]{:S(2)}, u32[]{:S(2)}) async-start(f32[3,32,96]{2,0,1:T(4,128)} %copy.42), calls=%async_computation.1 | async-start | bytes 131072 | tf_op jit(solution)/shard_map/all_to_all | solution.py:164
  59.3 0.6 copy-start.11
  116.9 4.6 %copy-start.9 = (s32[2,32,96]{2,0,1:T(2,128)S(1)}, s32[2,32,96]{2,0,1:T(2,128)}, u32[]{:S(2)}) copy-start(s32[2,32,96]{2,0,1:T(2,128)} %copy-done.8) | copy-start | bytes 73732
  122.5 7.0 %collective-permute-start.3 = (bf16[3,1,1,256,128]{4,3,2,1,0:T(8,128)(2,1)S(1)}, bf16[3,1,1,256,128]{4,3,2,1,0:T(8,128)(2,1)S(1)}, u32[]{:S(2)}, u32[]{:S(2)}) collective-permute-start(bf16[3,1,1,256,128]{4,3,2,1,0:T(8,128)(2,1)S(1)} %pad_maximum_fusion.4), channel_id=1, source_target_pairs={{8,0},{16,8},{24,16},{0,24},{9,1},{17,9},{25,17},{1,25},{10,2},{18... | collective-permute-start | bytes 589832 | tf_op jit(solution)/shard_map/ppermute | solution.py:21
  125.0 8.0 %collective-permute-start.2 = (bf16[3,1,1,256,128]{4,3,2,1,0:T(8,128)(2,1)S(1)}, bf16[3,1,1,256,128]{4,3,2,1,0:T(8,128)(2,1)S(1)}, u32[]{:S(2)}, u32[]{:S(2)}) collective-permute-start(bf16[3,1,1,256,128]{4,3,2,1,0:T(8,128)(2,1)S(1)} %pad_maximum_fusion.4), channel_id=1, source_target_pairs={{0,8},{8,16},{16,24},{24,0},{1,9},{9,17},{17,25},{25,1},{2,10},{10... | collective-permute-start | bytes 589832 | tf_op jit(solution)/shard_map/ppermute | solution.py:20
  133.9 14.7 %collective-permute-start.5 = (bf16[3,3,1,256,128]{4,3,2,1,0:T(8,128)(2,1)S(1)}, bf16[3,3,1,256,128]{4,3,2,1,0:T(8,128)(2,1)S(1)}, u32[]{:S(2)}, u32[]{:S(2)}) collective-permute-start(bf16[3,3,1,256,128]{4,3,2,1,0:T(8,128)(2,1)S(1)} %pad_maximum_fusion.3), channel_id=1, source_target_pairs={{1,0},{2,1},{3,2},{4,3},{5,4},{6,5},{7,6},{0,7},{9,8},{10,9},{11,1... | collective-permute-start | bytes 1769480 | tf_op jit(solution)/shard_map/ppermute | solution.py:21
  136.5 15.3 %collective-permute-start.4 = (bf16[3,3,1,256,128]{4,3,2,1,0:T(8,128)(2,1)S(1)}, bf16[3,3,1,256,128]{4,3,2,1,0:T(8,128)(2,1)S(1)}, u32[]{:S(2)}, u32[]{:S(2)}) collective-permute-start(bf16[3,3,1,256,128]{4,3,2,1,0:T(8,128)(2,1)S(1)} %pad_maximum_fusion.3), channel_id=1, source_target_pairs={{0,1},{1,2},{2,3},{3,4},{4,5},{5,6},{6,7},{7,0},{8,9},{9,10},{10,1... | collective-permute-start | bytes 1769480 | tf_op jit(solution)/shard_map/ppermute | solution.py:20
  152.8 0.7 copy-start.12
  153.5 9.2 %copy-start.10 = (bf16[128,512]{1,0:T(8,128)(2,1)S(1)}, bf16[128,512]{1,0:T(8,128)(2,1)}, u32[]{:S(2)}) copy-start(bf16[128,512]{1,0:T(8,128)(2,1)} %param.25) | copy-start | bytes 393220
  162.7 1.0 copy-start.23
  162.7 1.0 copy-start.25
  163.7 6.5 %copy-start.21 = (bf16[512,512]{1,0:T(8,128)(2,1)S(1)}, bf16[512,512]{1,0:T(8,128)(2,1)}, u32[]{:S(2)}) copy-start(bf16[512,512]{1,0:T(8,128)(2,1)} %param.27) | copy-start | bytes 1572868
  163.7 11.1 %slice-start = ((s8[7077888]{0:T(1024)(128)(4,1)}), s8[2883584]{0:T(1024)(128)(4,1)S(1)}, s32[]{:S(2)}) async-start(s8[7077888]{0:T(1024)(128)(4,1)} %bitcast.115), calls=%async_computation.4 | async-start | bytes 5767168
  170.2 2.7 copy-start.7
  170.2 4.6 %slice-start.1 = ((s8[7077888]{0:T(1024)(128)(4,1)}), s8[4194304]{0:T(1024)(128)(4,1)S(1)}, s32[]{:S(2)}) async-start(s8[7077888]{0:T(1024)(128)(4,1)} %bitcast.115), calls=%async_computation.5 | async-start | bytes 8388608
  172.9 1.8 copy-start.4
  172.9 1.9 copy-start.18
  172.9 1.9 copy-start.19
  174.7 4.8 %copy-start.3 = (f32[3072,384]{1,0:T(8,128)}, f32[3072,384]{1,0:T(8,128)S(1)}, u32[]{:S(2)}) copy-start(f32[3072,384]{1,0:T(8,128)S(1)} %fusion.68) | copy-start | bytes 14155780
  184.2 59.5 %all-to-all-start.3 = ((bf16[3,32,96,128]{3,2,0,1:T(8,128)(2,1)}), bf16[3,32,96,128]{3,2,0,1:T(8,128)(2,1)S(1)}, u32[]{:S(2)}, u32[]{:S(2)}) async-start(bf16[3,32,96,128]{3,2,0,1:T(8,128)(2,1)} %pad_maximum_fusion), calls=%async_computation.3 | async-start | bytes 4718592 | tf_op jit(solution)/shard_map/all_to_all | solution.py:200
  188.9 5.8 %copy-start.5 = (bf16[3072,512]{1,0:T(8,128)(2,1)S(1)}, bf16[3072,512]{1,0:T(8,128)(2,1)}, u32[]{:S(2)}) copy-start(bf16[3072,512]{1,0:T(8,128)(2,1)} %copy-done.4) | copy-start | bytes 9437188
  189.0 5.8 %copy-start.6 = (bf16[3072,128]{1,0:T(8,128)(2,1)S(1)}, bf16[3072,128]{1,0:T(8,128)(2,1)}, u32[]{:S(2)}) copy-start(bf16[3072,128]{1,0:T(8,128)(2,1)} %get-tuple-element.21) | copy-start | bytes 2359300
  189.0 5.8 %copy-start.22 = (bf16[384,512]{1,0:T(8,128)(2,1)S(1)}, bf16[384,512]{1,0:T(8,128)(2,1)}, u32[]{:S(2)}) copy-start(bf16[384,512]{1,0:T(8,128)(2,1)} %param.29) | copy-start | bytes 1179652
  189.0 5.8 %copy-start.24 = (f32[512]{0:T(512)S(1)}, f32[512]{0:T(512)}, u32[]{:S(2)}) copy-start(f32[512]{0:T(512)} %param.31) | copy-start | bytes 6148
  243.8 6.9 %copy-start.15 = (s32[2048,1]{0,1:T(1,128)S(1)}, s32[2048,1]{0,1:T(1,128)}, u32[]{:S(2)}) copy-start(s32[2048,1]{0,1:T(1,128)} %copy-done.14) | copy-start | bytes 24580
  243.8 78.3 %all-to-all-start.2 = ((bf16[1,32,96,512]{3,2,0,1:T(8,128)(2,1)}), bf16[1,32,96,512]{3,2,0,1:T(8,128)(2,1)}, u32[]{:S(2)}, u32[]{:S(2)}) async-start(bf16[1,32,96,512]{3,2,0,1:T(8,128)(2,1)} %bitcast.124), calls=%async_computation.2 | async-start | bytes 6291456 | tf_op jit(solution)/shard_map/all_to_all | solution.py:193
  322.1 11.7 %copy-start.1 = (bf16[1024,9,128]{2,0,1:T(8,128)(2,1)S(1)}, bf16[1024,9,128]{2,0,1:T(8,128)(2,1)}, u32[]{:S(2)}) copy-start(bf16[1024,9,128]{2,0,1:T(8,128)(2,1)} %param.17) | copy-start | bytes 7077892
where the time goes:
time: 338 us; the launch traced here: 334 us
  local copies, waits for them, and re-layouts  122 us (36%)
  waiting for transfers between devices  101 us (30%)
  other arithmetic  45.5 us (13%)
  starting transfers between devices  40.2 us (12%)
  matrix products  23.5 us (7%)
    gather x1, local copies, waits for them, and re-layouts, local(): atom_env[center_rows]  45.1 us
    all_to_all x1, waiting for transfers between devices, local(): lax.all_to_all(vector_far.reshape(3, owners, capacity, channels), ('gy',...  43.7 us
    all_to_all x1, waiting for transfers between devices, local(): lax.all_to_all(latent_far.reshape(1, owners, capacity, -1), ('gy', 'gz'),...  35.5 us
    scatter-add x1, other arithmetic, local(): jax.ops.segment_sum(energy_far, center_rows, num_segments=atoms_here)  22.5 us
    ppermute x3, waiting for transfers between devices, with_halo(): after = lax.ppermute(leading, axis, down)  14.7 us
    gather x1, local copies, waits for them, and re-layouts, local(): latent_out = back_latent.reshape(owners * capacity, -1)[slot]  11.7 us
    all_to_all x1, starting transfers between devices, side_by_side(): lax.all_to_all(both, axis, split_axis=split_dim, concat_axis=concat_dim,...  11.2 us
    all_to_all x1, starting transfers between devices, local(): lax.all_to_all(placed.reshape(3, owners, capacity), ('gy', 'gz'), split_a...  9.37 us
  transfers between devices with their start and end apart: 10, of which 6 were waited for; matrix products, arithmetic and copies ran while one was open for 43% of the time, Pallas kernels for 0%

commit v1 on v0

v1 whole, which is shorter than its diff:
```python
import functools

import jax
import jax.numpy as jnp
from jax import lax
from jax.experimental import pallas as pl
from jax.experimental.pallas import tpu as pltpu
from jax.sharding import PartitionSpec as P

MESH = pl.DeviceIdType.MESH
F32 = jnp.float32
BF16 = jnp.bfloat16
GX, GY, GZ = 8, 4, 8
OWN = GY * GZ
CAP = 96
PAIRS = 2048
ATOMS = 1024
EXPORT = 256
CH = 128
LAT = 512
WIDTH = LAT + 3 * CH
ROWS = GY * CAP
SPACING = 6.0 / 7.0
R2, R3, R5, R15 = 2.0**0.5, 3.0**0.5, 5.0**0.5, 15.0**0.5

PEERS = [(dy, dz) for dz in range(GZ) for dy in range(GY) if (dy, dz) != (0, 0)]
CELLS = [(s // 9 - 1, s // 3 % 3 - 1, s % 3 - 1) for s in range(27)]
NEAR = [s for s in range(27) if s != 13]


def iota(shape, dim):
    return lax.broadcasted_iota(jnp.int32, shape, dim)


def parts(v):
    hi = v.astype(BF16)
    rest = v - hi.astype(F32)
    mid = rest.astype(BF16)
    lo = (rest - mid.astype(F32)).astype(BF16)
    return hi, mid, lo


def dot(a, b):
    return jnp.dot(a, b, preferred_element_type=F32)


def dot_t(a, b):
    return lax.dot_general(a, b, (((1,), (1,)), ((), ())), preferred_element_type=F32)


def wrapped(v, n):
    return lax.rem(v + n, n)


def request_kernel(
    count_ref,
    owner_ref,
    center_ref,
    neigh_ref,
    vec_ref,
    export_ref,
    feat_ref,
    req_ref,
    halo_ref,
    slot_ref,
    cidx_ref,
    nidx_ref,
    out_scr,
    exp_scr,
    req_send,
    req_recv,
    halo_send,
    halo_recv,
):
    x, y, z = lax.axis_index("gx"), lax.axis_index("gy"), lax.axis_index("gz")
    me = y * GZ + z
    barrier = pltpu.get_barrier_semaphore()
    for dy, dz in PEERS:
        pl.semaphore_signal(
            barrier,
            inc=1,
            device_id=(x, wrapped(y + dy, GY), wrapped(z + dz, GZ)),
            device_id_type=MESH,
        )
    for s in NEAR:
        ox, oy, oz = CELLS[s]
        pl.semaphore_signal(
            barrier,
            inc=1,
            device_id=(wrapped(x - ox, GX), wrapped(y - oy, GY), wrapped(z - oz, GZ)),
            device_id_type=MESH,
        )

    index8 = jnp.broadcast_to(export_ref[...].astype(F32), (8, EXPORT))
    index_col = jnp.transpose(index8)[:, :1]
    pick = jnp.where(index_col == iota((EXPORT, ATOMS), 1).astype(F32), 1.0, 0.0).astype(BF16)
    exp_scr[...] = dot(pick, feat_ref[...]).astype(BF16)

    owner = owner_ref[...]
    member = jnp.where(owner == iota((OWN, PAIRS), 0), 1.0, 0.0)
    member_b = member.astype(BF16)
    block = 256
    before = jnp.where(iota((block, block), 0) < iota((block, block), 1), 1.0, 0.0).astype(BF16)
    running = jnp.zeros((OWN, 1), F32)
    pieces = []
    for b in range(PAIRS // block):
        cut = member_b[:, b * block : (b + 1) * block]
        pieces.append(dot(cut, before) + running)
        running = running + jnp.sum(
            member[:, b * block : (b + 1) * block], axis=1, keepdims=True
        )
    earlier = jnp.concatenate(pieces, axis=1)
    rank = jnp.sum(member * earlier, axis=0, keepdims=True)
    slot_ref[...] = jnp.broadcast_to(owner.astype(F32) * CAP + rank, (8, PAIRS))

    live = iota((1, PAIRS), 1) < count_ref[0]
    code = jnp.where(live, center_ref[...] + 1, 0).astype(F32)
    near = neigh_ref[...].astype(F32)
    field = iota((8, PAIRS), 0)
    values = jnp.where(field == 0, code, jnp.where(field == 1, near, 0.0))
    for m in range(3):
        values = jnp.where(field == 2 + m, vec_ref[m : m + 1, :], values)
    at_rank = jnp.where(rank == iota((CH, PAIRS), 0).astype(F32), 1.0, 0.0).astype(BF16)
    packed = jnp.zeros((OWN * 8, CH), F32)
    for part in parts(values):
        wide = part.astype(F32)
        stacked = jnp.concatenate(
            [jnp.where(owner == o, wide, 0.0) for o in range(OWN)], axis=0
        ).astype(BF16)
        packed = packed + dot_t(stacked, at_rank)
    code_row = jnp.where(iota((8, CH), 0) == 0, 1.0, 0.0)
    for o in range(OWN):
        out_scr[o] = packed[o * 8 : (o + 1) * 8] - code_row

    pl.semaphore_wait(barrier, len(PEERS) + len(NEAR))
    copies = []
    for k, (dy, dz) in enumerate(PEERS):
        ty, tz = wrapped(y + dy, GY), wrapped(z + dz, GZ)
        copies.append(
            pltpu.make_async_remote_copy(
                src_ref=out_scr.at[ty * GZ + tz],
                dst_ref=req_ref.at[me],
                send_sem=req_send.at[k],
                recv_sem=req_recv.at[k],
                device_id=(x, ty, tz),
                device_id_type=MESH,
            )
        )
    for k, s in enumerate(NEAR):
        ox, oy, oz = CELLS[s]
        copies.append(
            pltpu.make_async_remote_copy(
                src_ref=exp_scr,
                dst_ref=halo_ref.at[s],
                send_sem=halo_send.at[k],
                recv_sem=halo_recv.at[k],
                device_id=(wrapped(x - ox, GX), wrapped(y - oy, GY), wrapped(z - oz, GZ)),
                device_id_type=MESH,
            )
        )
    for c in copies:
        c.start()
    halo_ref[13] = exp_scr[...]
    req_ref[me] = out_scr[me]
    for c in copies:
        c.wait()
    got = req_ref[...]
    cidx_ref[...] = jnp.maximum(got[:, 0, :], 0.0).astype(jnp.int32)
    nidx_ref[...] = got[:, 1, :].astype(jnp.int32)


def silu(v):
    return v * jax.nn.sigmoid(v)


def owner_kernel(
    cidx_ref,
    nidx_ref,
    req_ref,
    feat_ref,
    halo_ref,
    env_ref,
    center_proj,
    neighbour_proj,
    radial_proj,
    hidden_proj,
    split_proj,
    scalar_proj,
    gain_ref,
    energy_proj,
    back_ref,
    energy_ref,
    table,
    hc_scr,
    hn_scr,
    env_scr,
    cols,
    geo,
    send,
    send_sem,
    recv_sem,
    self_sem,
):
    x, y, z = lax.axis_index("gx"), lax.axis_index("gy"), lax.axis_index("gz")
    me = y * GZ + z
    barrier = pltpu.get_barrier_semaphore()
    for dy, dz in PEERS:
        pl.semaphore_signal(
            barrier,
            inc=1,
            device_id=(x, wrapped(y + dy, GY), wrapped(z + dz, GZ)),
            device_id_type=MESH,
        )
    table[0:ATOMS, :] = feat_ref[...].astype(F32)
    for s in range(27):
        table[ATOMS + s * EXPORT : ATOMS + (s + 1) * EXPORT, :] = halo_ref[s].astype(F32)
    energy_ref[...] = jnp.zeros_like(energy_ref)
    gain = gain_ref[...]
    weight = jnp.broadcast_to(energy_proj[...], (8, LAT))
    w_hi, w_mid, w_lo = parts(weight)
    row8 = iota((8, LAT), 0)
    w_parts = jnp.where(
        row8 == 0,
        w_hi.astype(F32),
        jnp.where(row8 == 1, w_mid.astype(F32), jnp.where(row8 == 2, w_lo.astype(F32), 0.0)),
    ).astype(BF16)

    def target(step, dy):
        h = lax.rem(step + 1, GZ)
        half = (h + 1) // 2
        dz = jnp.where(lax.rem(h, 2) == 1, GZ - half, half)
        return wrapped(y + dy, GY), wrapped(z + dz, GZ)

    def copy_of(step, dy):
        ty, tz = target(step, dy)
        k = step * GY + dy
        return pltpu.make_async_remote_copy(
            src_ref=send.at[k],
            dst_ref=back_ref.at[me],
            send_sem=send_sem.at[k],
            recv_sem=recv_sem.at[k],
            device_id=(x, ty, tz),
            device_id_type=MESH,
        )

    def self_copy(step):
        return pltpu.make_async_copy(send.at[step * GY], back_ref.at[me], self_sem)

    def group(step, carry):
        for dy in range(GY):
            ty, tz = target(step, dy)
            s = ty * GZ + tz
            rows = req_ref[s]
            vx, vy, vz = rows[2:3], rows[3:4], rows[4:5]
            length = jnp.sqrt(vx * vx + vy * vy + vz * vz)
            scale = jnp.maximum(length, 1.0)
            ux, uy, uz = vx / scale, vy / scale, vz / scale
            geo[0:1, :] = rows[0:1]
            geo[1:2, :] = R3 * ux
            geo[2:3, :] = R3 * uy
            geo[3:4, :] = R3 * uz
            geo[4:5, :] = R15 * ux * uy
            geo[5:6, :] = R15 * uy * uz
            geo[6:7, :] = 0.5 * R5 * (2.0 * uz * uz - ux * ux - uy * uy)
            geo[7:8, :] = R15 * ux * uz
            geo[8:9, :] = 0.5 * R15 * (ux * ux - uy * uy)
            centres = iota((8, CH), 0).astype(F32) * SPACING
            ratio = (length - centres) / SPACING
            geo[16:24, :] = jnp.exp(-(ratio * ratio))
            cols[dy * CAP : (dy + 1) * CAP, 0:32] = jnp.transpose(geo[...])[0:CAP, :]

            def fetch(i, c):
                for u in range(8):
                    r = i * 8 + u
                    at = dy * CAP + r
                    ci = cidx_ref[s, r]
                    hc_scr[pl.ds(at, 1), :] = table[pl.ds(ci, 1), :]
                    hn_scr[pl.ds(at, 1), :] = table[pl.ds(nidx_ref[s, r], 1), :]
                    env_scr[pl.ds(at * 16, 9), :] = env_ref[ci].astype(F32)
                return c

            lax.fori_loop(0, CAP // 8, fetch, 0)

        def col(k):
            return cols[:, k : k + 1]

        def env(m):
            return env_scr[pl.ds(m, ROWS, stride=16), :]

        code = col(0)
        live = code >= 0.0
        radial = cols[:, 16:24]
        radial_hi = radial.astype(BF16)
        radial_lo = (radial - radial_hi.astype(F32)).astype(BF16)
        pre = dot(hc_scr[...].astype(BF16), center_proj[...])
        pre = pre + dot(hn_scr[...].astype(BF16), neighbour_proj[...])
        pre = pre + dot(radial_hi, radial_proj[...]) + dot(radial_lo, radial_proj[...])
        hidden = silu(pre).astype(BF16)
        latent = silu(dot(hidden, hidden_proj[...])).astype(BF16)
        mixed = dot(latent, split_proj[...])
        z0, z1, z2 = mixed[:, :CH], mixed[:, CH : 2 * CH], mixed[:, 2 * CH :]
        e0, ex, ey, ez = env(0), env(1), env(2), env(3)
        yx, yy, yz = col(1), col(2), col(3)
        first = (yx * ex + yy * ey + yz * ez) * (1.0 / R3)
        second = col(4) * env(4)
        for m in range(1, 5):
            second = second + col(4 + m) * env(4 + m)
        second = second * (1.0 / R5)
        invariants = jnp.concatenate([z0 * e0, z1 * first, z2 * second], axis=1).astype(BF16)
        update = silu(dot(invariants, scalar_proj[...]))
        out = jnp.where(live, latent.astype(F32) + update, 0.0).astype(BF16)
        a = gain[0:1] * z0
        b = gain[1:2] * z1 * e0
        c = (gain[2:3] * (1.0 / R2)) * z1
        ux = a * ex + b * yx + c * (yy * ez - yz * ey)
        uy = a * ey + b * yy + c * (yz * ex - yx * ez)
        uz = a * ez + b * yz + c * (yx * ey - yy * ex)
        vectors = [jnp.where(live, v, 0.0).astype(BF16) for v in (ux, uy, uz)]
        for dy in range(GY):
            k = step * GY + dy
            cut = slice(dy * CAP, (dy + 1) * CAP)
            send[k, :, 0:LAT] = out[cut]
            for m in range(3):
                send[k, :, LAT + m * CH : LAT + (m + 1) * CH] = vectors[m][cut]

        @pl.when(step == 0)
        def _():
            pl.semaphore_wait(barrier, len(PEERS))

        for dy in range(1, GY):
            copy_of(step, dy).start()

        @pl.when(step < GZ - 1)
        def _():
            copy_of(step, 0).start()

        @pl.when(step == GZ - 1)
        def _():
            self_copy(step).start()

        pair_energy = jnp.sum(dot_t(w_parts, out), axis=0, keepdims=True)
        e_hi, e_mid, e_lo = parts(jnp.broadcast_to(pair_energy, (8, ROWS)))
        row = iota((8, ROWS), 0)
        e_parts = jnp.where(
            row == 0,
            e_hi.astype(F32),
            jnp.where(row == 1, e_mid.astype(F32), jnp.where(row == 2, e_lo.astype(F32), 0.0)),
        ).astype(BF16)
        onehot = jnp.where(code == iota((ROWS, ATOMS), 1).astype(F32), 1.0, 0.0).astype(BF16)
        energy_ref[...] += dot(e_parts, onehot)
        return carry

    lax.fori_loop(0, GZ, group, 0)

    def finish(step, carry):
        for dy in range(1, GY):
            copy_of(step, dy).wait()

        @pl.when(step < GZ - 1)
        def _():
            copy_of(step, 0).wait()

        @pl.when(step == GZ - 1)
        def _():
            self_copy(step).wait()

        return carry

    lax.fori_loop(0, GZ, finish, 0)


def return_kernel(slot_ref, back_ref, latent_ref, vector_ref):
    col = jnp.transpose(slot_ref[...])[:, :1]
    pick = jnp.where(col == iota((256, OWN * CAP), 1).astype(F32), 1.0, 0.0).astype(BF16)
    got = dot(pick, back_ref[...]).astype(BF16)
    latent_ref[...] = got[:, :LAT]
    for m in range(3):
        vector_ref[m] = got[:, LAT + m * CH : LAT + (m + 1) * CH]


def vmem():
    return pl.BlockSpec(memory_space=pltpu.VMEM)


def smem():
    return pl.BlockSpec(memory_space=pltpu.SMEM)


def shaped(shape, dtype):
    return jax.ShapeDtypeStruct(shape, dtype)


def local(
    atom_feat,
    atom_env,
    export_index,
    pair_vec,
    pair_center,
    pair_owner,
    pair_neigh,
    pair_count,
    center_proj,
    neighbour_proj,
    radial_proj,
    hidden_proj,
    split_proj,
    scalar_proj,
    path_gain,
    energy_proj,
):
    req, halo, slot, cidx, nidx = pl.pallas_call(
        request_kernel,
        out_shape=(
            shaped((OWN, 8, CH), F32),
            shaped((27, EXPORT, CH), BF16),
            shaped((8, PAIRS), F32),
            shaped((OWN, CH), jnp.int32),
            shaped((OWN, CH), jnp.int32),
        ),
        in_specs=[smem()] + [vmem()] * 6,
        out_specs=tuple([vmem()] * 5),
        scratch_shapes=[
            pltpu.VMEM((OWN, 8, CH), F32),
            pltpu.VMEM((EXPORT, CH), BF16),
            pltpu.SemaphoreType.DMA((31,)),
            pltpu.SemaphoreType.DMA((31,)),
            pltpu.SemaphoreType.DMA((26,)),
            pltpu.SemaphoreType.DMA((26,)),
        ],
        compiler_params=pltpu.CompilerParams(collective_id=0, has_side_effects=True),
    )(
        pair_count,
        pair_owner.reshape(1, PAIRS),
        pair_center.reshape(1, PAIRS),
        pair_neigh.reshape(1, PAIRS),
        pair_vec,
        export_index.reshape(1, EXPORT),
        atom_feat,
    )
    back, energy = pl.pallas_call(
        owner_kernel,
        out_shape=(shaped((OWN, CAP, WIDTH), BF16), shaped((8, ATOMS), F32)),
        in_specs=[smem()] * 2 + [vmem()] * 12,
        out_specs=(pl.BlockSpec(memory_space=pl.ANY), vmem()),
        scratch_shapes=[
            pltpu.VMEM((ATOMS + 27 * EXPORT, CH), F32),
            pltpu.VMEM((ROWS, CH), F32),
            pltpu.VMEM((ROWS, CH), F32),
            pltpu.VMEM((ROWS * 16, CH), F32),
            pltpu.VMEM((ROWS, CH), F32),
            pltpu.VMEM((32, CH), F32),
            pltpu.VMEM((OWN, CAP, WIDTH), BF16),
            pltpu.SemaphoreType.DMA((OWN,)),
            pltpu.SemaphoreType.DMA((OWN,)),
            pltpu.SemaphoreType.DMA,
        ],
        compiler_params=pltpu.CompilerParams(
            collective_id=1, has_side_effects=True, vmem_limit_bytes=56 * 1024 * 1024
        ),
    )(
        cidx,
        nidx,
        req,
        atom_feat,
        halo,
        atom_env,
        center_proj,
        neighbour_proj,
        radial_proj,
        hidden_proj,
        split_proj,
        scalar_proj,
        path_gain,
        energy_proj.reshape(1, LAT),
    )
    latent, vector = pl.pallas_call(
        return_kernel,
        grid=(PAIRS // 256,),
        out_shape=(shaped((PAIRS, LAT), BF16), shaped((3, PAIRS, CH), BF16)),
        in_specs=[
            pl.BlockSpec((8, 256), lambda i: (0, i)),
            pl.BlockSpec((OWN * CAP, WIDTH), lambda i: (0, 0)),
        ],
        out_specs=(
            pl.BlockSpec((256, LAT), lambda i: (i, 0)),
            pl.BlockSpec((3, 256, CH), lambda i: (0, i, 0)),
        ),
        compiler_params=pltpu.CompilerParams(vmem_limit_bytes=40 * 1024 * 1024),
    )(slot, back.reshape(OWN * CAP, WIDTH))
    return (latent, vector, jnp.sum(energy, axis=0))


def solution(mesh):
    rows = ("gx", "gy", "gz")
    placed = (
        P(rows, None),
        P(rows, None, None),
        P(rows),
        P(None, rows),
        P(rows),
        P(rows, None),
        P(rows),
        P(rows),
    ) + (P(),) * 8
    return jax.shard_map(
        local,
        mesh=mesh,
        in_specs=placed,
        out_specs=(P(rows, None), P(None, rows, None), P(rows)),
        check_vma=False,
    )
```

time: 338 us -> 199 us (0.59); the launches traced: 334 us -> 199 us
  Pallas kernels: 0 us -> 189 us
  local copies, waits for them, and re-layouts: 122 us -> 8 us
  waiting for transfers between devices: 101 us -> 0 us
  other arithmetic: 45.5 us -> 0.6 us
  starting transfers between devices: 40.2 us -> 0 us
  matrix products: 23.5 us -> 0 us
    pallas_call x0 -> x3, Pallas kernels: none -> 189 us  [the longest x1 141 us: local(): pl.pallas_call(owner_kernel, out_shape=(shaped((OWN, CAP, WIDTH), BF16),...]
    gather x6 -> x0, local copies, waits for them, and re-layouts: 85.5 us -> none  [the longest x1 45.1 us: local(): atom_env[center_rows]]
    all_to_all x4 -> x0, waiting for transfers between devices: 79.2 us -> none  [the longest x1 43.7 us: local(): lax.all_to_all(vector_far.reshape(3, owners, capacity, channels), ('gy',...]
    all_to_all x4 -> x0, starting transfers between devices: 32.2 us -> none  [the longest x1 11.2 us: side_by_side(): lax.all_to_all(both, axis, split_axis=split_dim, concat_axis=concat_dim,...]
    dot_general x7 -> x0, matrix products: 23.5 us -> none  [the longest x1 6.5 us: pair_block(): jnp.dot(radial, radial_proj.astype(jnp.float32), precision=lax.Precision....]
    scatter x3 -> x0, local copies, waits for them, and re-layouts: 23.4 us -> none  [the longest x1 8.22 us: local(): jnp.zeros((owners * capacity,), jnp.int32).at[slot].set(pair_neigh)]
    scatter-add x1 -> x0, other arithmetic: 22.5 us -> none  [local(): jax.ops.segment_sum(energy_far, center_rows, num_segments=atoms_here)]
    ppermute x6 -> x0, waiting for transfers between devices: 21.3 us -> none  [the longest x3 14.7 us: with_halo(): after = lax.ppermute(leading, axis, down)]
  transfers between devices with their start and end apart: 10 -> 0, of which waited for: 6 -> 0; matrix products, arithmetic and copies ran while one was open for 43% -> 0% of each run, Pallas kernels for 0% -> 0%
where the time goes in v1:
time: 199 us
  Pallas kernels  189 us (95%)
  local copies, waits for them, and re-layouts  8 us (4%)
    pallas_call x1, Pallas kernels, local(): pl.pallas_call(owner_kernel, out_shape=(shaped((OWN, CAP, WIDTH), BF16),...  141 us
    pallas_call x1, Pallas kernels, local(): pl.pallas_call(request_kernel, out_shape=(shaped((OWN, 8, CH), F32), shap...  30.9 us
    pallas_call x1, Pallas kernels, local(): pl.pallas_call(return_kernel, grid=(PAIRS // 256,), out_shape=(shaped((PA...  16.8 us
    unnamed x7, local copies, waits for them, and re-layouts  8 us

profile of v1, /device:TPU:7, one launch (start us, length us, event | category | flops | bytes accessed | tf_op | source)
XLA Modules:
  0.0 198.8 jit_solution(7258264118137901500)
XLA Ops:
  1.3 30.9 %shard_map.175 = (f32[32,8,128]{2,1,0:T(8,128)}, bf16[27,256,128]{2,1,0:T(8,128)(2,1)}, f32[8,2048]{1,0:T(8,128)}, s32[32,128]{1,0:T(8,128)}, s32[32,128]{1,0:T(8,128)}) custom-call(s32[1]{0:T(128)S(6)} %copy.20.count_ref, s32[1,2048]{1,0:T(1,128)} %bitcast.7, s32[1,2048]{1,0:T(1,128)} %bitcast.8, s32[1,2048]{1,0:T(1,128)} %bitcast.9, f32[3,2048]{1,0:T(4,128)} %vec_ref.1, ...), custom_call_target="tpu_custom_call" | custom-call | tf_op jit(solution)/shard_map/pallas_call | solution.py:411
  32.2 5.4 %copy.19.env_ref = bf16[1024,9,128]{2,1,0:T(8,128)(2,1)} copy(bf16[1024,9,128]{2,0,1:T(8,128)(2,1)} %param.17) | data formatting | bytes 4718592 | tf_op args[1]
  37.6 0.0 copy-start.1
  37.6 141.2 %shard_map.176 = (bf16[32,96,896]{2,1,0:T(8,128)(2,1)}, f32[8,1024]{1,0:T(8,128)}) custom-call(s32[32,128]{1,0:T(8,128)} %get-tuple-element.13.cidx_ref, s32[32,128]{1,0:T(8,128)} %get-tuple-element.14.nidx_ref, f32[32,8,128]{2,1,0:T(8,128)} %get-tuple-element.15.req_ref, bf16[1024,128]{1,0:T(8,128)(2,1)} %feat_ref.3, ...), custom_call_target="tpu_custom_call" | custom-call | tf_op jit(solution)/shard_map/pallas_call | solution.py:440
  178.8 0.0 copy-done.1
  178.9 0.0 copy-start
  178.9 2.6 %copy-done = bf16[32,96,896]{2,1,0:T(8,128)(2,1)S(1)} copy-done((bf16[32,96,896]{2,1,0:T(8,128)(2,1)S(1)}, bf16[32,96,896]{2,1,0:T(8,128)(2,1)}, u32[]{:S(2)}) %copy-start) | copy-done | bytes 5505048
  181.4 0.0 copy-start.2
  181.4 16.8 %shard_map.177 = (bf16[2048,512]{1,0:T(8,128)(2,1)}, bf16[3,2048,128]{2,1,0:T(8,128)(2,1)}) custom-call(f32[8,2048]{1,0:T(8,128)S(1)} %copy-done.1, bf16[3072,896]{1,0:T(8,128)(2,1)S(1)} %bitcast.6), custom_call_target="tpu_custom_call" | custom-call | tf_op jit(solution)/shard_map/pallas_call | solution.py:476
  198.2 0.0 copy-done.2
  198.2 0.6 reduce_sum.9
Async XLA Ops:
  37.6 141.2 %copy-start.1 = (f32[8,2048]{1,0:T(8,128)S(1)}, f32[8,2048]{1,0:T(8,128)}, u32[]{:S(2)}) copy-start(f32[8,2048]{1,0:T(8,128)} %get-tuple-element.12.slot_ref) | copy-start | bytes 196612
  178.9 2.6 %copy-start = (bf16[32,96,896]{2,1,0:T(8,128)(2,1)S(1)}, bf16[32,96,896]{2,1,0:T(8,128)(2,1)}, u32[]{:S(2)}) copy-start(bf16[32,96,896]{2,1,0:T(8,128)(2,1)} %get-tuple-element.17) | copy-start | bytes 16515076
  181.4 16.8 %copy-start.2 = (f32[8,1024]{1,0:T(8,128)S(1)}, f32[8,1024]{1,0:T(8,128)}, u32[]{:S(2)}) copy-start(f32[8,1024]{1,0:T(8,128)} %get-tuple-element.20) | copy-start | bytes 98308
